TPU v7x, 32 devices: a whole 2x2x4 slice. The times are simulated.
32 devices in a mesh: dom: 4 (over z), col: 8 (over y, x, core).
Axes of the slice: x: 2, y: 2, z: 4, core: 2. Of those that a mesh axis runs over, the one named last changes fastest.
Arguments:
- rhs_interior: bfloat16 [4, 48, 8192], P('dom', 'col'), may hold values from -6 to 6
- interior_inv: bfloat16 [4, 8192, 8192], P('dom', None, 'col'), may hold values from -0.0625 to 0.0625
- coupling: bfloat16 [4, 8192, 768], P('dom', 'col'), may hold values from -0.0625 to 0.0625
- rhs_interface: bfloat16 [48, 8192], P('col', 'dom'), may hold values from -6 to 6
- block_ids: int32 [4, 6], P('dom'), may hold values from 0 to 63, as said below
- interface_inv: bfloat16 [8192, 8192], P('dom', 'col'), may hold values from -0.0625 to 0.0625
Outputs:
- interior_solution: bfloat16 [4, 48, 8192], P('dom', None, 'col')
- interface_solution: bfloat16 [48, 8192], P('col')
Inputs may be any that keep to these rules, and one draw needn't show every extreme that they name: `block_ids`: each row names 6 different blocks.
All inputs are finite; a program needn't handle non-finite values.
Results may differ from a plain program's by a relative error of at most 0.025.
Values may be sent and summed in bfloat16 or wider, within the bound.
A program may use at most 64 MiB of HBM per device.

v0:
```python
import jax
import jax.numpy as jnp
from jax import lax
from jax.sharding import PartitionSpec as P

G = 8192
BS = 128


def per_device(rhs_interior, interior_inv, coupling, rhs_interface, block_ids, interface_inv):
    rhs_local = rhs_interior[0]
    inverse = interior_inv[0]
    couple = coupling[0]
    blocks = block_ids[0]
    row_count = rhs_local.shape[0]
    block_count = blocks.shape[0]
    nblocks = G // BS
    onehot = (blocks[:, None] == jnp.arange(nblocks, dtype=jnp.int32)[None, :]).astype(jnp.float32)
    interior_step = jnp.dot(
        lax.all_gather(rhs_local, "col", axis=0, tiled=True),
        inverse,
        preferred_element_type=jnp.float32,
    ).astype(jnp.bfloat16)
    contribution = lax.psum_scatter(
        jnp.dot(interior_step, couple, preferred_element_type=jnp.float32).astype(jnp.bfloat16),
        "col",
        scatter_dimension=0,
        tiled=True,
    ).astype(jnp.float32)
    placed = jnp.einsum(
        "kb,rks->rbs", onehot, contribution.reshape(row_count, block_count, BS)
    ).reshape(row_count, G)
    summed = lax.psum_scatter(
        placed.astype(jnp.bfloat16), "dom", scatter_dimension=1, tiled=True
    ).astype(jnp.float32)
    reduced = (rhs_interface.astype(jnp.float32) - summed).astype(jnp.bfloat16)
    partial_solution = jnp.dot(
        lax.all_gather(reduced, "col", axis=0, tiled=True),
        interface_inv,
        preferred_element_type=jnp.float32,
    )
    column_total = lax.psum(partial_solution.astype(jnp.bfloat16), "dom")
    solution = lax.all_to_all(column_total, "col", split_axis=0, concat_axis=1, tiled=True)
    local_solution = jnp.einsum(
        "kb,rbs->rks",
        onehot.astype(jnp.bfloat16),
        solution.reshape(row_count, nblocks, BS),
        preferred_element_type=jnp.float32,
    )
    local_solution = local_solution.reshape(row_count, block_count * BS).astype(jnp.bfloat16)
    every_solution = lax.all_gather(local_solution, "col", axis=0, tiled=True)
    correction = jnp.einsum("rl,il->ri", every_solution, couple, preferred_element_type=jnp.float32)
    rhs_columns = lax.all_to_all(rhs_local, "col", split_axis=1, concat_axis=0, tiled=True)
    interior_rhs = (rhs_columns.astype(jnp.float32) - correction).astype(jnp.bfloat16)
    result = jnp.dot(
        lax.all_gather(interior_rhs, "col", axis=1, tiled=True),
        inverse,
        preferred_element_type=jnp.float32,
    )
    interior_solution = result.astype(jnp.bfloat16)[None]
    return (interior_solution, solution)


def solution(mesh):
    placed = (
        P("dom", "col", None),
        P("dom", None, "col"),
        P("dom", "col", None),
        P("col", "dom"),
        P("dom", None),
        P("dom", "col"),
    )
    return jax.shard_map(
        per_device,
        mesh=mesh,
        in_specs=placed,
        out_specs=(P("dom", None, "col"), P("col", None)),
        check_vma=False,
    )
```

profile of v0, /device:TPU:0, one launch (start us, length us, event | category | flops | bytes accessed | tf_op | source)
XLA Modules:
  0.0 168.0 jit_solution(9237124908893844768)
XLA Ops:
  7.2 0.0 reduce-scatter.4.cloned.1.call-start
  7.2 1.2 copy.15
  8.4 14.6 %all-gather = bf16[1,48,8192]{2,0,1:T(2,128)(2,1)S(1)} all-gather(bf16[1,6,8192]{2,0,1:T(2,128)(2,1)S(1)} %copy.15), channel_id=2, replica_groups=mesh['dom'=4,'col'=8] {'col'}, dimensions={1}, use_global_device_ids=true | all-gather | bytes 884736 | tf_op jit(solution)/shard_map/all_gather | solution.py:20
  23.0 9.5 %fusion.21 = bf16[48,768]{1,0:T(8,128)(2,1)S(1)} fusion(bf16[1,1024,768]{2,1,0:T(8,128)(2,1)S(1)} %copy-done, bf16[1,8192,1024]{2,1,0:T(8,128)(2,1)} %param.7, bf16[1,48,8192]{2,0,1:T(2,128)(2,1)S(1)} %all-gather), kind=kOutput, calls=%fused_computation.14 | convolution fusion | flops 880889856 | bytes 19210240 | tf_op jit(solution)/shard_map/dot_general | solution.py:25
  32.6 14.5 %fusion = bf16[8,768]{1,0:T(8,128)(2,1)S(1)} fusion(bf16[48,768]{1,0:T(8,128)(2,1)S(1)} %fusion.21), kind=kCustom, calls=%all-reduce-scatter | all-reduce-scatter fusion | flops 49153 | bytes 86528
  47.1 1.3 collective-permute-start
  48.4 2.0 %collective-permute-start.1 = (bf16[6,768]{1,0:T(8,128)(2,1)S(1)}, bf16[6,768]{1,0:T(8,128)(2,1)S(1)}, u32[]{:S(2)}, u32[]{:S(2)}) collective-permute-start(bf16[6,768]{1,0:T(8,128)(2,1)S(1)} %slice), channel_id=1, source_target_pairs={{0,2},{1,3},{2,4},{3,5},{4,6},{5,7},{8,10},{9,11},{10,12},{11,13},... | collective-permute-start | bytes 27656
  50.4 0.6 dynamic-slice.4
  51.7 0.1 collective-permute-done.1
  51.8 0.2 concatenate
  52.1 0.3 fusion.24
  52.4 0.7 copy.25
  53.1 0.0 reduce-scatter.4.cloned.1.call-update
  53.1 0.0 all-reduce.4.cloned.1.call-start
  53.2 23.2 %reduce-scatter.4.cloned.1.call-done = bf16[6,2048]{1,0:T(8,128)(2,1)} async-done(((bf16[6,8192]{1,0:T(8,128)(2,1)}), bf16[6,2048]{1,0:T(8,128)(2,1)}) %reduce-scatter.4.cloned.1.call-update) | async-done | bytes 24592 | tf_op jit(solution)/shard_map/reduce_scatter | solution.py:33
  76.4 0.8 fusion.35
  77.1 9.3 %all-gather.1 = bf16[8,6,2048]{2,1,0:T(8,128)(2,1)S(1)} all-gather(bf16[1,6,2048]{2,1,0:T(8,128)(2,1)S(1)} %fusion.35), channel_id=1, replica_groups=mesh['dom'=4,'col'=8] {'col'}, dimensions={0}, use_global_device_ids=true | all-gather | bytes 221184 | tf_op jit(solution)/shard_map/all_gather | solution.py:38
  86.4 0.1 reshape.30
  86.5 3.0 %convolution_convert_fusion = bf16[48,1024]{1,0:T(8,128)(2,1)S(1)} fusion(bf16[48,2048]{1,0:T(8,128)(2,1)S(1)} %reshape.30, bf16[2048,1024]{1,0:T(8,128)(2,1)} %param.11), kind=kOutput, calls=%fused_computation.12 | convolution fusion | flops 201375744 | bytes 4489216 | tf_op jit(solution)/shard_map/dot_general | solution.py:37
  89.5 0.7 all_to_all.26
  90.2 0.0 all-reduce.4.cloned.1.call-update
  90.2 8.0 %all_to_all.32 = bf16[6,8,1024]{2,0,1:T(8,128)(2,1)S(1)} all-to-all(bf16[6,8,1024]{2,0,1:T(8,128)(2,1)S(1)} %bitcast.65), channel_id=1, replica_groups=mesh['dom'=4,'col'=8] {'col'}, dimensions={1} | all-to-all | bytes 196608 | tf_op jit(solution)/shard_map/all_to_all | solution.py:53
  98.3 24.0 %all-reduce.4.cloned.1.call-done = bf16[8,6,1024]{2,1,0:T(8,128)(2,1)} async-done(((bf16[8,6,1024]{2,1,0:T(8,128)(2,1)}), bf16[8,6,1024]{2,1,0:T(8,128)(2,1)}) %all-reduce.4.cloned.1.call-update) | async-done | bytes 98320 | tf_op jit(solution)/shard_map/psum | solution.py:42
  122.3 3.6 %all-to-all-start.1 = ((bf16[8,6,1024]{2,1,0:T(8,128)(2,1)}), bf16[8,6,1024]{2,1,0:T(8,128)(2,1)S(1)}, u32[]{:S(2)}, u32[]{:S(2)}) async-start(bf16[8,6,1024]{2,1,0:T(8,128)(2,1)} %all-reduce.4.cloned.1.call-done), calls=%async_computation.2 | async-start | bytes 262144 | tf_op jit(solution)/shard_map/all_to_all | solution.py:43
  126.0 5.4 %all-to-all-done.1 = bf16[8,6,1024]{2,1,0:T(8,128)(2,1)S(1)} async-done(((bf16[8,6,1024]{2,1,0:T(8,128)(2,1)}), bf16[8,6,1024]{2,1,0:T(8,128)(2,1)S(1)}, u32[]{:S(2)}, u32[]{:S(2)}) %all-to-all-start.1) | async-done | bytes 98336 | tf_op jit(solution)/shard_map/all_to_all | solution.py:43
  131.4 0.1 copy.16
  131.5 0.2 fusion.28
  131.7 8.3 %all-gather.2 = bf16[8,6,768]{2,1,0:T(8,128)(2,1)S(1)} all-gather(bf16[1,6,768]{2,1,0:T(8,128)(2,1)S(1)} %reshape.31), channel_id=1, replica_groups=mesh['dom'=4,'col'=8] {'col'}, dimensions={0}, use_global_device_ids=true | all-gather | bytes 82944 | tf_op jit(solution)/shard_map/all_gather | solution.py:51
  140.1 0.6 fusion.12
  140.6 10.4 %all_gather.15 = bf16[48,8192]{1,0:T(8,128)(2,1)S(1)} all-gather(bf16[48,1024]{1,0:T(8,128)(2,1)S(1)} %fusion.12), channel_id=1, replica_groups=mesh['dom'=4,'col'=8] {'col'}, dimensions={1}, use_global_device_ids=true | all-gather | bytes 884736 | tf_op jit(solution)/shard_map/all_gather | solution.py:56
  151.0 9.5 %fusion.25 = bf16[1,48,1024]{2,1,0:T(8,128)(2,1)} fusion(bf16[48,8192]{1,0:T(8,128)(2,1)S(1)} %all_gather.15, bf16[1,8192,1024]{2,1,0:T(8,128)(2,1)} %param.7), kind=kOutput, calls=%fused_computation.16 | convolution fusion | flops 805355520 | bytes 17661952 | tf_op jit(solution)/shard_map/dot_general | solution.py:55
  160.5 0.7 copy.28
  (19 shorter events, 0.2 us)
Async XLA Ops:
  7.2 15.9 %copy-start = (bf16[1,1024,768]{2,1,0:T(8,128)(2,1)S(1)}, bf16[1,1024,768]{2,1,0:T(8,128)(2,1)}, u32[]{:S(2)}) copy-start(bf16[1,1024,768]{2,1,0:T(8,128)(2,1)} %param.8) | copy-start | bytes 4718596
  7.2 69.2 %reduce-scatter.4.cloned.1.call-start = ((), (), s32[]{:S(2)}) async-start(), calls=%async_computation.3 | async-start | bytes 163840 | tf_op jit(solution)/shard_map/reduce_scatter | solution.py:33
  23.0 27.4 %copy-start.3 = (u32[32]{0:T(128)S(1)}, u32[32]{0:T(128)}, u32[]{:S(2)}) copy-start(u32[32]{0:T(128)} %constant.7) | copy-start | bytes 388
  23.0 29.0 %copy-start.4 = (s32[1,6]{1,0:T(1,128)S(1)}, s32[1,6]{1,0:T(1,128)}, u32[]{:S(2)}) copy-start(s32[1,6]{1,0:T(1,128)} %param.10) | copy-start | bytes 76
  23.0 53.3 %copy-start.2 = (bf16[6,2048]{1,0:T(8,128)(2,1)S(1)}, bf16[6,2048]{1,0:T(8,128)(2,1)}, u32[]{:S(2)}) copy-start(bf16[6,2048]{1,0:T(8,128)(2,1)} %param.9) | copy-start | bytes 73732
  32.6 57.6 %copy-start.1 = (bf16[1,6,8192]{2,1,0:T(8,128)(2,1)S(1)}, bf16[1,6,8192]{2,1,0:T(8,128)(2,1)}, u32[]{:S(2)}) copy-start(bf16[1,6,8192]{2,1,0:T(8,128)(2,1)} %param.6) | copy-start | bytes 294916
  47.1 4.7 %collective-permute-start = (bf16[8,768]{1,0:T(8,128)(2,1)S(1)}, bf16[8,768]{1,0:T(8,128)(2,1)S(1)}, u32[]{:S(2)}, u32[]{:S(2)}) collective-permute-start(bf16[8,768]{1,0:T(8,128)(2,1)S(1)} %fusion), channel_id=1, source_target_pairs={{0,1},{1,2},{2,3},{3,4},{4,5},{5,6},{6,7},{8,9},{9,10},{10,11},{11... | collective-permute-start | bytes 36872
  48.4 3.4 %collective-permute-start.1 = (bf16[6,768]{1,0:T(8,128)(2,1)S(1)}, bf16[6,768]{1,0:T(8,128)(2,1)S(1)}, u32[]{:S(2)}, u32[]{:S(2)}) collective-permute-start(bf16[6,768]{1,0:T(8,128)(2,1)S(1)} %slice), channel_id=1, source_target_pairs={{0,2},{1,3},{2,4},{3,5},{4,6},{5,7},{8,10},{9,11},{10,12},{11,13},... | collective-permute-start | bytes 27656
  53.1 69.1 %all-reduce.4.cloned.1.call-start = ((), (), s32[]{:S(2)}) async-start(), calls=%async_computation.4 | async-start | bytes 262144 | tf_op jit(solution)/shard_map/psum | solution.py:42
  122.3 9.1 %all-to-all-start.1 = ((bf16[8,6,1024]{2,1,0:T(8,128)(2,1)}), bf16[8,6,1024]{2,1,0:T(8,128)(2,1)S(1)}, u32[]{:S(2)}, u32[]{:S(2)}) async-start(bf16[8,6,1024]{2,1,0:T(8,128)(2,1)} %all-reduce.4.cloned.1.call-done), calls=%async_computation.2 | async-start | bytes 262144 | tf_op jit(solution)/shard_map/all_to_all | solution.py:43
Sparse Core Ops, SparseCore 0:
  53.3 23.0 reduce-scatter.3
  90.3 31.8 all-reduce.3
where the time goes:
time: 169 us; the launch traced here: 168 us
  blocking collectives  65 us (38%)
  waiting for transfers between devices  52.8 us (31%)
  matrix products  23.1 us (14%)
  between operations  14.9 us (9%)
  starting transfers between devices  7.03 us (4%)
  local copies, waits for them, and re-layouts  4.39 us (3%)
    psum x1, waiting for transfers between devices, per_device(): column_total = lax.psum(partial_solution.astype(jnp.bfloat16), 'dom')  24 us
    reduce_scatter x1, waiting for transfers between devices, per_device(): lax.psum_scatter(placed.astype(jnp.bfloat16), 'dom', scatter_dimension=1,...  23.2 us
    all_gather x1, blocking collectives, per_device(): lax.all_gather(rhs_local, 'col', axis=0, tiled=True)  14.6 us
    unnamed x1, blocking collectives  14.5 us
    all_gather x1, blocking collectives, per_device(): lax.all_gather(interior_rhs, 'col', axis=1, tiled=True)  10.4 us
    dot_general x1, matrix products, per_device(): jnp.dot(interior_step, couple, preferred_element_type=jnp.float32)  9.54 us
    dot_general x1, matrix products, per_device(): jnp.dot(lax.all_gather(interior_rhs, 'col', axis=1, tiled=True), inverse,...  9.46 us
    all_gather x1, blocking collectives, per_device(): lax.all_gather(reduced, 'col', axis=0, tiled=True)  9.25 us
  transfers between devices with their start and end apart: 5, of which 4 were waited for; matrix products, arithmetic and copies ran while one was open for 0% of the time, Pallas kernels for 0%

commit v1 on v0

v1 whole, which is shorter than its diff:
```python
import functools

import jax
import jax.numpy as jnp
from jax import lax
from jax.experimental import pallas as pl
from jax.experimental.pallas import tpu as pltpu
from jax.sharding import PartitionSpec as P

BF = jnp.bfloat16
F32 = jnp.float32
MESH = pl.DeviceIdType.MESH
LANES = 128
CHUNKS = 4


def partner(me, o, n):
    total, bit = 0, 1
    while bit < n:
        total = total + lax.rem(lax.div(me, bit) + (o // bit) % 2, 2) * bit
        bit *= 2
    return total


def kernel(C, D, ids_ref, rhs_ref, ri_ref, inv_hbm, cp_hbm, ii_hbm, out_ref, sol_ref,
           inv, cp, ii, gath, xf, xg, xl, rhsl, idsb, s2, r2, g3, acc3, g4, s5, r5,
           s6, r6, g7, x8, r9, g10, stepb,
           ld, ss, rs, s1sem, r1sem):
    c = lax.axis_index("col")
    d = lax.axis_index("dom")
    rl, ni = rhs_ref.shape
    nl = inv.shape[1]
    li = cp.shape[1]
    gl = ii.shape[0]
    gc = ii.shape[1]
    kb = li // LANES
    w = ni // CHUNKS

    loads = []
    for j in range(CHUNKS):
        rows = pl.ds(j * w, w)
        loads.append(pltpu.make_async_copy(inv_hbm.at[rows, :], inv.at[rows, :], ld.at[j]))
    loads.append(pltpu.make_async_copy(cp_hbm, cp, ld.at[CHUNKS]))
    loads.append(pltpu.make_async_copy(ii_hbm, ii, ld.at[CHUNKS + 1]))
    for copy in loads:
        copy.start()

    barrier = pltpu.get_barrier_semaphore()
    for o in range(1, C):
        pl.semaphore_signal(barrier, inc=1, device_id={"col": partner(c, o, C)}, device_id_type=MESH)
    for o in range(1, D):
        pl.semaphore_signal(barrier, inc=1, device_id={"dom": partner(d, o, D)}, device_id_type=MESH)
    pl.semaphore_wait(barrier, C - 1 + D - 1)

    def send(src, dst, phase, o, axis, target):
        copy = pltpu.make_async_remote_copy(
            src_ref=src, dst_ref=dst, send_sem=ss.at[phase, o], recv_sem=rs.at[phase, o],
            device_id={axis: target}, device_id_type=MESH)
        copy.start()
        return copy

    done = []

    first = []
    for j in range(CHUNKS):
        cols = pl.ds(j * w, w)
        row = []
        for o in range(1, C):
            copy = pltpu.make_async_remote_copy(
                src_ref=rhs_ref.at[:, cols], dst_ref=gath.at[c, :, cols],
                send_sem=s1sem.at[j, o], recv_sem=r1sem.at[j, o],
                device_id={"col": partner(c, o, C)}, device_id_type=MESH)
            copy.start()
            row.append(copy)
        first.append(row)
        done += row
    gath[c] = rhs_ref[...]
    for k in range(kb):
        idsb[d, :, k * LANES:(k + 1) * LANES] = jnp.full((8, LANES), ids_ref[0, k], jnp.int32)
    idcopies = [send(idsb.at[d], idsb.at[d], 0, o, "dom", partner(d, o, D)) for o in range(1, D)]
    done += idcopies

    acc = None
    for j in range(CHUNKS):
        for copy in first[j]:
            copy.wait_recv()
        for q in range(C):
            xf[q * rl:(q + 1) * rl, :] = gath[q, :, j * w:(j + 1) * w].astype(F32)
        loads[j].wait()
        part = jnp.dot(xf[...].astype(BF), inv[j * w:(j + 1) * w, :], preferred_element_type=F32)
        acc = part if acc is None else acc + part
    stepb[...] = acc.astype(BF)

    loads[CHUNKS].wait()
    con = jnp.dot(stepb[...], cp[...], preferred_element_type=F32)
    for q in range(C):
        s2[q] = con[q * rl:(q + 1) * rl, :].astype(BF)
    copies = []
    for o in range(1, C):
        t = partner(c, o, C)
        copies.append(send(s2.at[t], r2.at[c], 1, o, "col", t))
    done += copies
    r2[c] = s2[c]
    for q in range(C):
        rhsl[q * rl:(q + 1) * rl, :] = gath[q, :, pl.ds(pl.multiple_of(c * nl, LANES), nl)].astype(F32)
    for copy in copies:
        copy.wait_recv()
    total = r2[0].astype(F32)
    for q in range(1, C):
        total = total + r2[q].astype(F32)

    g3[d] = total.astype(BF)
    copies = [send(g3.at[d], g3.at[d], 2, o, "dom", partner(d, o, D)) for o in range(1, D)]
    done += copies
    acc3[...] = ri_ref[...].astype(F32)
    for copy in idcopies:
        copy.wait_recv()
    for copy in copies:
        copy.wait_recv()
    base = d * (gl // LANES)

    def place(s, carry):
        ids = [idsb[s, 0:rl, k * LANES:(k + 1) * LANES] - base for k in range(kb)]
        val = [g3[s, :, k * LANES:(k + 1) * LANES].astype(F32) for k in range(kb)]
        for j in range(gl // LANES):
            part = jnp.zeros((rl, LANES), F32)
            for k in range(kb):
                part = jnp.where(ids[k] == j, val[k], part)
            at = slice(j * LANES, (j + 1) * LANES)
            acc3[:, at] = acc3[:, at] - part
        return carry

    lax.fori_loop(0, D, place, 0)

    g4[c] = acc3[...].astype(BF)
    copies = [send(g4.at[c], g4.at[c], 3, o, "col", partner(c, o, C)) for o in range(1, C)]
    done += copies
    loads[CHUNKS + 1].wait()
    for copy in copies:
        copy.wait_recv()
    for q in range(C):
        xg[q * rl:(q + 1) * rl, :] = g4[q].astype(F32)
    part = jnp.dot(xg[...].astype(BF), ii[...], preferred_element_type=F32)

    for q in range(C):
        s5[q] = part[q * rl:(q + 1) * rl, :].astype(BF)
    copies = []
    for o in range(1, C):
        t = partner(c, o, C)
        copies.append(send(s5.at[t], r5.at[c], 4, o, "col", t))
    done += copies
    r5[c] = s5[c]
    for copy in copies:
        copy.wait_recv()

    per = gc // LANES

    def pick(s, carry):
        ids = [idsb[s, 0:rl, k * LANES:(k + 1) * LANES] for k in range(kb)]
        got = [jnp.zeros((rl, LANES), F32) for k in range(kb)]
        for q in range(C):
            for j in range(per):
                block = r5[q, :, j * LANES:(j + 1) * LANES].astype(F32)
                got = [jnp.where(ids[k] == q * per + j, block, got[k]) for k in range(kb)]
        for k in range(kb):
            s6[s, :, k * LANES:(k + 1) * LANES] = got[k].astype(BF)
        return carry

    lax.fori_loop(0, D, pick, 0)
    copies = []
    for o in range(1, D):
        t = partner(d, o, D)
        copies.append(send(s6.at[t], r6.at[d], 5, o, "dom", t))
    done += copies
    span = C // D
    ninth = []
    for o in range(1, D):
        t = partner(d, o, D)
        ninth.append(send(r5.at[pl.ds(t * span, span)], r9.at[d], 6, o, "dom", t))
    done += ninth
    r6[d] = s6[d]
    for q in range(span):
        r9[d, q] = r5[d * span + q]
    for copy in copies:
        copy.wait_recv()
    total = r6[0].astype(F32)
    for s in range(1, D):
        total = total + r6[s].astype(F32)

    g7[c] = total.astype(BF)
    copies = [send(g7.at[c], g7.at[c], 7, o, "col", partner(c, o, C)) for o in range(1, C)]
    done += copies
    for copy in copies:
        copy.wait_recv()
    for q in range(C):
        xl[q * rl:(q + 1) * rl, :] = g7[q].astype(F32)
    corr = lax.dot_general(xl[...].astype(BF), cp[...], (((1,), (1,)), ((), ())), preferred_element_type=F32)

    x8[c] = (rhsl[...] - corr).astype(BF)
    copies = [send(x8.at[c], x8.at[c], 8, o, "col", partner(c, o, C)) for o in range(1, C)]
    done += copies

    for copy in ninth:
        copy.wait_recv()
    for q in range(span):
        total = r9[0, q].astype(F32)
        for s in range(1, D):
            total = total + r9[s, q].astype(F32)
        g10[d, q] = total.astype(BF)
    tenth = [send(g10.at[d], g10.at[d], 9, o, "dom", partner(d, o, D)) for o in range(1, D)]
    done += tenth

    acc = None
    for o in range(C):
        q = partner(c, o, C)
        if o > 0:
            copies[o - 1].wait_recv()
        part = jnp.dot(x8[q], inv[pl.ds(pl.multiple_of(q * nl, LANES), nl), :], preferred_element_type=F32)
        acc = part if acc is None else acc + part
    out_ref[...] = acc.astype(BF)

    for copy in tenth:
        copy.wait_recv()
    for s in range(D):
        for q in range(span):
            at = (s * span + q) * gc
            sol_ref[:, at:at + gc] = g10[s, q]
    for copy in done:
        copy.wait_send()


def per_device(C, D, rhs_interior, interior_inv, coupling, rhs_interface, block_ids, interface_inv):
    rl, ni = rhs_interior.shape[1:]
    nl = interior_inv.shape[2]
    li = coupling.shape[2]
    gl, gc = interface_inv.shape
    r = rl * C
    span = C // D
    vmem = pl.BlockSpec(memory_space=pltpu.VMEM)
    hbm = pl.BlockSpec(memory_space=pl.ANY)
    scratch = [
        pltpu.VMEM((ni, nl), BF), pltpu.VMEM((coupling.shape[1], li), BF), pltpu.VMEM((gl, gc), BF),
        pltpu.VMEM((C, rl, ni), BF),
        pltpu.VMEM((r, ni // CHUNKS), F32), pltpu.VMEM((r, gl), F32), pltpu.VMEM((r, li), F32),
        pltpu.VMEM((r, nl), F32),
        pltpu.VMEM((D, 8, li), jnp.int32),
        pltpu.VMEM((C, rl, li), BF), pltpu.VMEM((C, rl, li), BF),
        pltpu.VMEM((D, rl, li), BF), pltpu.VMEM((rl, gl), F32),
        pltpu.VMEM((C, rl, gl), BF),
        pltpu.VMEM((C, rl, gc), BF), pltpu.VMEM((C, rl, gc), BF),
        pltpu.VMEM((D, rl, li), BF), pltpu.VMEM((D, rl, li), BF),
        pltpu.VMEM((C, rl, li), BF),
        pltpu.VMEM((C, r, nl), BF),
        pltpu.VMEM((D, span, rl, gc), BF), pltpu.VMEM((D, span, rl, gc), BF),
        pltpu.VMEM((r, nl), BF),
        pltpu.SemaphoreType.DMA((CHUNKS + 2,)),
        pltpu.SemaphoreType.DMA((10, C)), pltpu.SemaphoreType.DMA((10, C)),
        pltpu.SemaphoreType.DMA((CHUNKS, C)), pltpu.SemaphoreType.DMA((CHUNKS, C)),
    ]
    out, sol = pl.pallas_call(
        functools.partial(kernel, C, D),
        out_shape=(jax.ShapeDtypeStruct((r, nl), BF), jax.ShapeDtypeStruct((rl, gc * C), BF)),
        in_specs=[pl.BlockSpec(memory_space=pltpu.SMEM), vmem, vmem, hbm, hbm, hbm],
        out_specs=(vmem, vmem),
        scratch_shapes=scratch,
        compiler_params=pltpu.CompilerParams(
            collective_id=0, has_side_effects=True, vmem_limit_bytes=60 * 1024 * 1024),
    )(block_ids, rhs_interior[0], rhs_interface, interior_inv[0], coupling[0], interface_inv)
    return out[None], sol


def solution(mesh):
    placed = (
        P("dom", "col", None),
        P("dom", None, "col"),
        P("dom", "col", None),
        P("col", "dom"),
        P("dom", None),
        P("dom", "col"),
    )
    return jax.shard_map(
        functools.partial(per_device, mesh.shape["col"], mesh.shape["dom"]),
        mesh=mesh,
        in_specs=placed,
        out_specs=(P("dom", None, "col"), P("col", None)),
        check_vma=False,
    )
```

time: 169 us -> 62.6 us (0.37)
  blocking collectives: 65 us -> 0 us
  Pallas kernels: 0 us -> 58.7 us
  waiting for transfers between devices: 52.8 us -> 0 us
  matrix products: 23.1 us -> 0 us
  between operations: 14.9 us -> 0.64 us
  starting transfers between devices: 7.03 us -> 0 us
    pallas_call x0 -> x1, Pallas kernels: none -> 58.7 us  [per_device(): pl.pallas_call(functools.partial(kernel, C, D), out_shape=(jax.ShapeDtype...]
    all_gather x4 -> x0, blocking collectives: 42.5 us -> none  [the longest x1 14.6 us: per_device(): lax.all_gather(rhs_local, 'col', axis=0, tiled=True)]
    psum x1 -> x0, waiting for transfers between devices: 24 us -> none  [per_device(): column_total = lax.psum(partial_solution.astype(jnp.bfloat16), 'dom')]
    reduce_scatter x1 -> x0, waiting for transfers between devices: 23.2 us -> none  [per_device(): lax.psum_scatter(placed.astype(jnp.bfloat16), 'dom', scatter_dimension=1,...]
    dot_general x6 -> x0, matrix products: 23.1 us -> none  [the longest x1 9.54 us: per_device(): jnp.dot(interior_step, couple, preferred_element_type=jnp.float32)]
    unnamed x1 -> x0, blocking collectives: 14.5 us -> none
    all_to_all x1 -> x0, blocking collectives: 8.04 us -> none  [per_device(): lax.all_to_all(rhs_local, 'col', split_axis=1, concat_axis=0, tiled=True)]
    all_to_all x1 -> x0, waiting for transfers between devices: 5.44 us -> none  [per_device(): lax.all_to_all(column_total, 'col', split_axis=0, concat_axis=1, tiled=True)]
  transfers between devices with their start and end apart: 5 -> 0, of which waited for: 4 -> 0; matrix products, arithmetic and copies ran while one was open for 0% -> 0% of each run, Pallas kernels for 0% -> 0%
where the time goes in v1:
time: 62.6 us; the launch traced here: 62.4 us
  Pallas kernels  58.7 us (94%)
  local copies, waits for them, and re-layouts  3.11 us (5%)
  between operations  0.64 us (1%)
    pallas_call x1, Pallas kernels, per_device(): pl.pallas_call(functools.partial(kernel, C, D), out_shape=(jax.ShapeDtype...  58.7 us
    unnamed x2, local copies, waits for them, and re-layouts  3.11 us

profile of v1, /device:TPU:0, one launch (start us, length us, event | category | flops | bytes accessed | tf_op | source)
XLA Modules:
  0.0 62.4 jit_solution(13638965886351107203)
XLA Ops:
  0.6 58.7 %shard_map.77 = (bf16[48,1024]{1,0:T(8,128)(2,1)}, bf16[6,8192]{1,0:T(8,128)(2,1)}) custom-call(s32[1,6]{1,0:T(1,128)} %ids_ref.1, bf16[6,8192]{1,0:T(8,128)(2,1)} %bitcast.6, bf16[6,2048]{1,0:T(8,128)(2,1)} %ri_ref.1, bf16[8192,1024]{1,0:T(8,128)(2,1)} %bitcast.4, bf16[1024,768]{1,0:T(8,128)(2,1)} %bitcast.5, bf16[2048,1024]{1,0:T(8,128)(2,1)} %ii_hbm.1), custom_call_target="tpu_custom_call" | custom-call | tf_op jit(solution)/shard_map/pallas_call | solution.py:260
  59.3 1.5 %copy.10 = bf16[1,48,1024]{2,1,0:T(8,128)(2,1)} copy(bf16[1,48,1024]{2,1,0:T(8,128)(2,1)} %bitcast.7) | data formatting | bytes 196608
  60.9 1.6 %copy.11 = bf16[6,8192]{1,0:T(8,128)(2,1)} copy(bf16[6,8192]{1,0:T(8,128)(2,1)} %get-tuple-element.9) | data formatting | bytes 196608

commit v2 on v1

--- a/solution.py
+++ b/solution.py
@@ -11,7 +11,8 @@
 F32 = jnp.float32
 MESH = pl.DeviceIdType.MESH
 LANES = 128
-CHUNKS = 4
+CHUNKS = 8
+HALVES = 2
 
 
 def partner(me, o, n):
@@ -25,7 +26,7 @@
 def kernel(C, D, ids_ref, rhs_ref, ri_ref, inv_hbm, cp_hbm, ii_hbm, out_ref, sol_ref,
            inv, cp, ii, gath, xf, xg, xl, rhsl, idsb, s2, r2, g3, acc3, g4, s5, r5,
            s6, r6, g7, x8, r9, g10, stepb,
-           ld, ss, rs, s1sem, r1sem):
+           ld, ss, rs, s1sem, r1sem, s8sem, r8sem):
     c = lax.axis_index("col")
     d = lax.axis_index("dom")
     rl, ni = rhs_ref.shape
@@ -61,34 +62,44 @@
 
     done = []
 
-    first = []
+    def part1(src, j, q, o, target):
+        cols = pl.ds(j * w, w)
+        copy = pltpu.make_async_remote_copy(
+            src_ref=src.at[:, cols], dst_ref=gath.at[q, :, cols],
+            send_sem=s1sem.at[j, o], recv_sem=r1sem.at[j, o],
+            device_id={"col": target}, device_id_type=MESH)
+        copy.start()
+        done.append(copy)
+        return copy
+
+    far, near = [], []
     for j in range(CHUNKS):
-        cols = pl.ds(j * w, w)
-        row = []
-        for o in range(1, C):
-            copy = pltpu.make_async_remote_copy(
-                src_ref=rhs_ref.at[:, cols], dst_ref=gath.at[c, :, cols],
-                send_sem=s1sem.at[j, o], recv_sem=r1sem.at[j, o],
-                device_id={"col": partner(c, o, C)}, device_id_type=MESH)
-            copy.start()
-            row.append(copy)
-        first.append(row)
-        done += row
+        far.append([part1(rhs_ref, j, c, o, partner(c, o, C)) for o in reversed(range(2, C, 2))])
+        near.append([part1(rhs_ref, j, c, 1, partner(c, 1, C))])
     gath[c] = rhs_ref[...]
     for k in range(kb):
         idsb[d, :, k * LANES:(k + 1) * LANES] = jnp.full((8, LANES), ids_ref[0, k], jnp.int32)
     idcopies = [send(idsb.at[d], idsb.at[d], 0, o, "dom", partner(d, o, D)) for o in range(1, D)]
     done += idcopies
 
-    acc = None
-    for j in range(CHUNKS):
-        for copy in first[j]:
+    def dot1(j, acc):
+        for copy in near[j]:
             copy.wait_recv()
         for q in range(C):
             xf[q * rl:(q + 1) * rl, :] = gath[q, :, j * w:(j + 1) * w].astype(F32)
         loads[j].wait()
         part = jnp.dot(xf[...].astype(BF), inv[j * w:(j + 1) * w, :], preferred_element_type=F32)
-        acc = part if acc is None else acc + part
+        return part if acc is None else acc + part
+
+    acc = None
+    for j in range(CHUNKS):
+        for copy, o in zip(far[j], reversed(range(2, C, 2))):
+            copy.wait_recv()
+            q = partner(c, o, C)
+            near[j].append(part1(gath.at[q], j, q, o + 1, partner(c, 1, C)))
+        if j > 0:
+            acc = dot1(j - 1, acc)
+    acc = dot1(CHUNKS - 1, acc)
     stepb[...] = acc.astype(BF)
 
     loads[CHUNKS].wait()
@@ -197,8 +208,22 @@
     corr = lax.dot_general(xl[...].astype(BF), cp[...], (((1,), (1,)), ((), ())), preferred_element_type=F32)
 
     x8[c] = (rhsl[...] - corr).astype(BF)
-    copies = [send(x8.at[c], x8.at[c], 8, o, "col", partner(c, o, C)) for o in range(1, C)]
-    done += copies
+    wide = nl // HALVES
+
+    def part8(h, q, o, target):
+        cols = pl.ds(h * wide, wide)
+        copy = pltpu.make_async_remote_copy(
+            src_ref=x8.at[q, :, cols], dst_ref=x8.at[q, :, cols],
+            send_sem=s8sem.at[h, o], recv_sem=r8sem.at[h, o],
+            device_id={"col": target}, device_id_type=MESH)
+        copy.start()
+        done.append(copy)
+        return copy
+
+    far, near = [], []
+    for h in range(HALVES):
+        far.append([part8(h, c, o, partner(c, o, C)) for o in reversed(range(2, C, 2))])
+    side = [part8(h, c, 1, partner(c, 1, C)) for h in range(HALVES)]
 
     for copy in ninth:
         copy.wait_recv()
@@ -210,13 +235,27 @@
     tenth = [send(g10.at[d], g10.at[d], 9, o, "dom", partner(d, o, D)) for o in range(1, D)]
     done += tenth
 
-    acc = None
-    for o in range(C):
+    def dot8(h, o):
         q = partner(c, o, C)
-        if o > 0:
-            copies[o - 1].wait_recv()
-        part = jnp.dot(x8[q], inv[pl.ds(pl.multiple_of(q * nl, LANES), nl), :], preferred_element_type=F32)
-        acc = part if acc is None else acc + part
+        rows = pl.ds(pl.multiple_of(q * nl + h * wide, LANES), wide)
+        return jnp.dot(x8[q, :, h * wide:(h + 1) * wide], inv[rows, :], preferred_element_type=F32)
+
+    acc = dot8(0, 0)
+    for h in range(1, HALVES):
+        acc = acc + dot8(h, 0)
+    for h in range(HALVES):
+        side[h].wait_recv()
+        acc = acc + dot8(h, 1)
+    order = list(reversed(range(2, C, 2)))
+    for h in range(HALVES):
+        for copy, o in zip(far[h], order):
+            copy.wait_recv()
+            near.append(part8(h, partner(c, o, C), o + 1, partner(c, 1, C)))
+            acc = acc + dot8(h, o)
+    for h in range(HALVES):
+        for i, o in enumerate(order):
+            near[h * len(order) + i].wait_recv()
+            acc = acc + dot8(h, o + 1)
     out_ref[...] = acc.astype(BF)
 
     for copy in tenth:
@@ -256,6 +295,7 @@
         pltpu.SemaphoreType.DMA((CHUNKS + 2,)),
         pltpu.SemaphoreType.DMA((10, C)), pltpu.SemaphoreType.DMA((10, C)),
         pltpu.SemaphoreType.DMA((CHUNKS, C)), pltpu.SemaphoreType.DMA((CHUNKS, C)),
+        pltpu.SemaphoreType.DMA((HALVES, C)), pltpu.SemaphoreType.DMA((HALVES, C)),
     ]
     out, sol = pl.pallas_call(
         functools.partial(kernel, C, D),

time: 62.6 us -> 58.8 us (0.939)
  Pallas kernels: 58.7 us -> 54.8 us
    pallas_call x1, Pallas kernels: 58.7 us -> 54.8 us  [per_device(): pl.pallas_call(functools.partial(kernel, C, D), out_shape=(jax.ShapeDtype...]
where the time goes in v2:
time: 58.8 us; the launch traced here: 58.6 us
  Pallas kernels  54.8 us (93%)
  local copies, waits for them, and re-layouts  3.11 us (5%)
  between operations  0.64 us (1%)
    pallas_call x1, Pallas kernels, per_device(): pl.pallas_call(functools.partial(kernel, C, D), out_shape=(jax.ShapeDtype...  54.8 us
    unnamed x2, local copies, waits for them, and re-layouts  3.11 us

profile of v2, /device:TPU:0, one launch (start us, length us, event | category | flops | bytes accessed | tf_op | source)
XLA Modules:
  0.0 58.6 jit_solution(16216479268807878003)
XLA Ops:
  0.6 54.8 %shard_map.77 = (bf16[48,1024]{1,0:T(8,128)(2,1)}, bf16[6,8192]{1,0:T(8,128)(2,1)}) custom-call(s32[1,6]{1,0:T(1,128)} %ids_ref.1, bf16[6,8192]{1,0:T(8,128)(2,1)} %bitcast.6, bf16[6,2048]{1,0:T(8,128)(2,1)} %ri_ref.1, bf16[8192,1024]{1,0:T(8,128)(2,1)} %bitcast.4, bf16[1024,768]{1,0:T(8,128)(2,1)} %bitcast.5, bf16[2048,1024]{1,0:T(8,128)(2,1)} %ii_hbm.1), custom_call_target="tpu_custom_call" | custom-call | tf_op jit(solution)/shard_map/pallas_call | solution.py:300
  55.5 1.5 %copy.10 = bf16[1,48,1024]{2,1,0:T(8,128)(2,1)} copy(bf16[1,48,1024]{2,1,0:T(8,128)(2,1)} %bitcast.7) | data formatting | bytes 196608
  57.0 1.6 %copy.11 = bf16[6,8192]{1,0:T(8,128)(2,1)} copy(bf16[6,8192]{1,0:T(8,128)(2,1)} %get-tuple-element.9) | data formatting | bytes 196608

commit v3 on v2

--- a/solution.py
+++ b/solution.py
@@ -23,13 +23,13 @@
     return total
 
 
-def kernel(C, D, ids_ref, rhs_ref, ri_ref, inv_hbm, cp_hbm, ii_hbm, out_ref, sol_ref,
-           inv, cp, ii, gath, xf, xg, xl, rhsl, idsb, s2, r2, g3, acc3, g4, s5, r5,
-           s6, r6, g7, x8, r9, g10, stepb,
-           ld, ss, rs, s1sem, r1sem, s8sem, r8sem):
+def kernel(C, D, ids_hbm, rhs_hbm, ri_hbm, inv_hbm, cp_hbm, ii_hbm, out_hbm, sol_hbm,
+           ids_ref, ri_ref, outb, inv, cp, ii, gath, xf, xg, xl, rhsl, idsb, s2, r2, g3, acc3, g4, s5, r5,
+           f6, s6, r6, g7, x8, r9, g10, stepb,
+           ld, st, ss, rs, s1sem, r1sem, s8sem, r8sem):
     c = lax.axis_index("col")
     d = lax.axis_index("dom")
-    rl, ni = rhs_ref.shape
+    rl, ni = rhs_hbm.shape
     nl = inv.shape[1]
     li = cp.shape[1]
     gl = ii.shape[0]
@@ -37,6 +37,12 @@
     kb = li // LANES
     w = ni // CHUNKS
 
+    rhs_load = pltpu.make_async_copy(rhs_hbm, gath.at[c], ld.at[CHUNKS + 2])
+    ids_load = pltpu.make_async_copy(ids_hbm, ids_ref, ld.at[CHUNKS + 3])
+    ri_load = pltpu.make_async_copy(ri_hbm, ri_ref, ld.at[CHUNKS + 4])
+    rhs_load.start()
+    ids_load.start()
+    ri_load.start()
     loads = []
     for j in range(CHUNKS):
         rows = pl.ds(j * w, w)
@@ -72,14 +78,15 @@
         done.append(copy)
         return copy
 
+    rhs_load.wait()
     far, near = [], []
     for j in range(CHUNKS):
-        far.append([part1(rhs_ref, j, c, o, partner(c, o, C)) for o in reversed(range(2, C, 2))])
-        near.append([part1(rhs_ref, j, c, 1, partner(c, 1, C))])
-    gath[c] = rhs_ref[...]
+        far.append([part1(gath.at[c], j, c, o, partner(c, o, C)) for o in reversed(range(2, C, 2))])
+        near.append([part1(gath.at[c], j, c, 1, partner(c, 1, C))])
+    ids_load.wait()
     for k in range(kb):
         idsb[d, :, k * LANES:(k + 1) * LANES] = jnp.full((8, LANES), ids_ref[0, k], jnp.int32)
-    idcopies = [send(idsb.at[d], idsb.at[d], 0, o, "dom", partner(d, o, D)) for o in range(1, D)]
+    idcopies = [send(idsb.at[d], idsb.at[d], 0, o, "dom", partner(d, o, D)) for o in reversed(range(1, D))]
     done += idcopies
 
     def dot1(j, acc):
@@ -107,7 +114,7 @@
     for q in range(C):
         s2[q] = con[q * rl:(q + 1) * rl, :].astype(BF)
     copies = []
-    for o in range(1, C):
+    for o in reversed(range(1, C)):
         t = partner(c, o, C)
         copies.append(send(s2.at[t], r2.at[c], 1, o, "col", t))
     done += copies
@@ -121,8 +128,9 @@
         total = total + r2[q].astype(F32)
 
     g3[d] = total.astype(BF)
-    copies = [send(g3.at[d], g3.at[d], 2, o, "dom", partner(d, o, D)) for o in range(1, D)]
-    done += copies
+    copies = [send(g3.at[d], g3.at[d], 2, o, "dom", partner(d, o, D)) for o in reversed(range(1, D))]
+    done += copies
+    ri_load.wait()
     acc3[...] = ri_ref[...].astype(F32)
     for copy in idcopies:
         copy.wait_recv()
@@ -144,48 +152,60 @@
     lax.fori_loop(0, D, place, 0)
 
     g4[c] = acc3[...].astype(BF)
-    copies = [send(g4.at[c], g4.at[c], 3, o, "col", partner(c, o, C)) for o in range(1, C)]
-    done += copies
+    half = gl // 2
+    sides = []
+    for h in range(2):
+        cols = pl.ds(h * half, half)
+        sides.append([send(g4.at[c, :, cols], g4.at[c, :, cols], 3 + 7 * h, o, "col", partner(c, o, C))
+                      for o in reversed(range(1, C))])
+        done += sides[h]
     loads[CHUNKS + 1].wait()
-    for copy in copies:
-        copy.wait_recv()
-    for q in range(C):
-        xg[q * rl:(q + 1) * rl, :] = g4[q].astype(F32)
-    part = jnp.dot(xg[...].astype(BF), ii[...], preferred_element_type=F32)
+    part = None
+    for h in range(2):
+        for copy in sides[h]:
+            copy.wait_recv()
+        for q in range(C):
+            xg[q * rl:(q + 1) * rl, :] = g4[q, :, h * half:(h + 1) * half].astype(F32)
+        piece = jnp.dot(xg[...].astype(BF), ii[h * half:(h + 1) * half, :], preferred_element_type=F32)
+        part = piece if part is None else part + piece
 
     for q in range(C):
         s5[q] = part[q * rl:(q + 1) * rl, :].astype(BF)
     copies = []
-    for o in range(1, C):
+    for o in reversed(range(1, C)):
         t = partner(c, o, C)
         copies.append(send(s5.at[t], r5.at[c], 4, o, "col", t))
     done += copies
     r5[c] = s5[c]
-    for copy in copies:
-        copy.wait_recv()
 
     per = gc // LANES
-
-    def pick(s, carry):
-        ids = [idsb[s, 0:rl, k * LANES:(k + 1) * LANES] for k in range(kb)]
-        got = [jnp.zeros((rl, LANES), F32) for k in range(kb)]
-        for q in range(C):
-            for j in range(per):
-                block = r5[q, :, j * LANES:(j + 1) * LANES].astype(F32)
-                got = [jnp.where(ids[k] == q * per + j, block, got[k]) for k in range(kb)]
-        for k in range(kb):
-            s6[s, :, k * LANES:(k + 1) * LANES] = got[k].astype(BF)
-        return carry
-
-    lax.fori_loop(0, D, pick, 0)
+    for o in range(C):
+        if o > 0:
+            copies[C - 1 - o].wait_recv()
+        q = partner(c, o, C)
+
+        def pick(s, carry):
+            blocks = [r5[q, :, j * LANES:(j + 1) * LANES].astype(F32) for j in range(per)]
+            for k in range(kb):
+                at = slice(k * LANES, (k + 1) * LANES)
+                ids = idsb[s, 0:rl, at] - q * per
+                got = jnp.zeros((rl, LANES), F32) if o == 0 else f6[s, :, at]
+                for j in range(per):
+                    got = jnp.where(ids == j, blocks[j], got)
+                f6[s, :, at] = got
+            return carry
+
+        lax.fori_loop(0, D, pick, 0)
+    for s in range(D):
+        s6[s] = f6[s].astype(BF)
     copies = []
-    for o in range(1, D):
+    for o in reversed(range(1, D)):
         t = partner(d, o, D)
         copies.append(send(s6.at[t], r6.at[d], 5, o, "dom", t))
     done += copies
     span = C // D
     ninth = []
-    for o in range(1, D):
+    for o in reversed(range(1, D)):
         t = partner(d, o, D)
         ninth.append(send(r5.at[pl.ds(t * span, span)], r9.at[d], 6, o, "dom", t))
     done += ninth
@@ -199,7 +219,7 @@
         total = total + r6[s].astype(F32)
 
     g7[c] = total.astype(BF)
-    copies = [send(g7.at[c], g7.at[c], 7, o, "col", partner(c, o, C)) for o in range(1, C)]
+    copies = [send(g7.at[c], g7.at[c], 7, o, "col", partner(c, o, C)) for o in reversed(range(1, C))]
     done += copies
     for copy in copies:
         copy.wait_recv()
@@ -232,7 +252,7 @@
         for s in range(1, D):
             total = total + r9[s, q].astype(F32)
         g10[d, q] = total.astype(BF)
-    tenth = [send(g10.at[d], g10.at[d], 9, o, "dom", partner(d, o, D)) for o in range(1, D)]
+    tenth = [send(g10.at[d], g10.at[d], 9, o, "dom", partner(d, o, D)) for o in reversed(range(1, D))]
     done += tenth
 
     def dot8(h, o):
@@ -252,20 +272,39 @@
             copy.wait_recv()
             near.append(part8(h, partner(c, o, C), o + 1, partner(c, 1, C)))
             acc = acc + dot8(h, o)
+    stores = []
+    for copy in tenth:
+        copy.wait_recv()
+    for s in range(D):
+        for q in range(span):
+            n = s * span + q
+            store = pltpu.make_async_copy(g10.at[s, q], sol_hbm.at[:, pl.ds(n * gc, gc)], st.at[n])
+            store.start()
+            stores.append(store)
     for h in range(HALVES):
         for i, o in enumerate(order):
             near[h * len(order) + i].wait_recv()
             acc = acc + dot8(h, o + 1)
-    out_ref[...] = acc.astype(BF)
-
-    for copy in tenth:
-        copy.wait_recv()
-    for s in range(D):
-        for q in range(span):
-            at = (s * span + q) * gc
-            sol_ref[:, at:at + gc] = g10[s, q]
+    outb[...] = acc.astype(BF)
+    stores.append(pltpu.make_async_copy(outb, out_hbm, st.at[C]))
+    stores[-1].start()
+
+    for store in stores:
+        store.wait()
     for copy in done:
         copy.wait_send()
+
+
+def keep(a_hbm, b_hbm, a_out, b_out, a_buf, b_buf, sem):
+    first = [pltpu.make_async_copy(a_hbm, a_buf, sem.at[0]), pltpu.make_async_copy(b_hbm, b_buf, sem.at[1])]
+    then = [pltpu.make_async_copy(a_buf, a_out, sem.at[2]), pltpu.make_async_copy(b_buf, b_out, sem.at[3])]
+    for copy in first:
+        copy.start()
+    for copy, after in zip(first, then):
+        copy.wait()
+        after.start()
+    for copy in then:
+        copy.wait()
 
 
 def per_device(C, D, rhs_interior, interior_inv, coupling, rhs_interface, block_ids, interface_inv):
@@ -275,37 +314,46 @@
     gl, gc = interface_inv.shape
     r = rl * C
     span = C // D
-    vmem = pl.BlockSpec(memory_space=pltpu.VMEM)
+    ids_shape = block_ids.shape
     hbm = pl.BlockSpec(memory_space=pl.ANY)
     scratch = [
+        pltpu.SMEM(ids_shape, jnp.int32), pltpu.VMEM((rl, gl), BF), pltpu.VMEM((r, nl), BF),
         pltpu.VMEM((ni, nl), BF), pltpu.VMEM((coupling.shape[1], li), BF), pltpu.VMEM((gl, gc), BF),
         pltpu.VMEM((C, rl, ni), BF),
-        pltpu.VMEM((r, ni // CHUNKS), F32), pltpu.VMEM((r, gl), F32), pltpu.VMEM((r, li), F32),
+        pltpu.VMEM((r, ni // CHUNKS), F32), pltpu.VMEM((r, gl // 2), F32), pltpu.VMEM((r, li), F32),
         pltpu.VMEM((r, nl), F32),
         pltpu.VMEM((D, 8, li), jnp.int32),
         pltpu.VMEM((C, rl, li), BF), pltpu.VMEM((C, rl, li), BF),
         pltpu.VMEM((D, rl, li), BF), pltpu.VMEM((rl, gl), F32),
         pltpu.VMEM((C, rl, gl), BF),
         pltpu.VMEM((C, rl, gc), BF), pltpu.VMEM((C, rl, gc), BF),
+        pltpu.VMEM((D, rl, li), F32),
         pltpu.VMEM((D, rl, li), BF), pltpu.VMEM((D, rl, li), BF),
         pltpu.VMEM((C, rl, li), BF),
         pltpu.VMEM((C, r, nl), BF),
         pltpu.VMEM((D, span, rl, gc), BF), pltpu.VMEM((D, span, rl, gc), BF),
         pltpu.VMEM((r, nl), BF),
-        pltpu.SemaphoreType.DMA((CHUNKS + 2,)),
-        pltpu.SemaphoreType.DMA((10, C)), pltpu.SemaphoreType.DMA((10, C)),
+        pltpu.SemaphoreType.DMA((CHUNKS + 5,)), pltpu.SemaphoreType.DMA((C + 1,)),
+        pltpu.SemaphoreType.DMA((11, C)), pltpu.SemaphoreType.DMA((11, C)),
         pltpu.SemaphoreType.DMA((CHUNKS, C)), pltpu.SemaphoreType.DMA((CHUNKS, C)),
         pltpu.SemaphoreType.DMA((HALVES, C)), pltpu.SemaphoreType.DMA((HALVES, C)),
     ]
     out, sol = pl.pallas_call(
         functools.partial(kernel, C, D),
         out_shape=(jax.ShapeDtypeStruct((r, nl), BF), jax.ShapeDtypeStruct((rl, gc * C), BF)),
-        in_specs=[pl.BlockSpec(memory_space=pltpu.SMEM), vmem, vmem, hbm, hbm, hbm],
-        out_specs=(vmem, vmem),
+        in_specs=[hbm] * 6,
+        out_specs=(hbm, hbm),
         scratch_shapes=scratch,
         compiler_params=pltpu.CompilerParams(
             collective_id=0, has_side_effects=True, vmem_limit_bytes=60 * 1024 * 1024),
     )(block_ids, rhs_interior[0], rhs_interface, interior_inv[0], coupling[0], interface_inv)
+    out, sol = pl.pallas_call(
+        keep,
+        out_shape=(jax.ShapeDtypeStruct(out.shape, BF), jax.ShapeDtypeStruct(sol.shape, BF)),
+        in_specs=[hbm, hbm],
+        out_specs=(hbm, hbm),
+        scratch_shapes=[pltpu.VMEM(out.shape, BF), pltpu.VMEM(sol.shape, BF), pltpu.SemaphoreType.DMA((4,))],
+    )(out, sol)
     return out[None], sol
 
 

time: 58.8 us -> 55.6 us (0.946)
  local copies, waits for them, and re-layouts: 3.11 us -> 0 us
    unnamed x2 -> x0, local copies, waits for them, and re-layouts: 3.11 us -> none
    pallas_call x1, Pallas kernels: 54.8 us -> 53.2 us  [per_device(): pl.pallas_call(functools.partial(kernel, C, D), out_shape=(jax.ShapeDtype...]
    pallas_call x0 -> x1, Pallas kernels: none -> 1.64 us  [per_device(): pl.pallas_call(keep, out_shape=(jax.ShapeDtypeStruct(out.shape, BF), jax....]
where the time goes in v3:
time: 55.6 us; the launch traced here: 55.5 us
  Pallas kernels  54.8 us (99%)
  between operations  0.64 us (1%)
    pallas_call x1, Pallas kernels, per_device(): pl.pallas_call(functools.partial(kernel, C, D), out_shape=(jax.ShapeDtype...  53.2 us
    pallas_call x1, Pallas kernels, per_device(): pl.pallas_call(keep, out_shape=(jax.ShapeDtypeStruct(out.shape, BF), jax....  1.64 us

profile of v3, /device:TPU:0, one launch (start us, length us, event | category | flops | bytes accessed | tf_op | source)
XLA Modules:
  0.0 55.5 jit_solution(4949466174671689591)
XLA Ops:
  0.6 53.2 %shard_map.77 = (bf16[48,1024]{1,0:T(8,128)(2,1)}, bf16[6,8192]{1,0:T(8,128)(2,1)}) custom-call(s32[1,6]{1,0:T(1,128)} %ids_hbm.1, bf16[6,8192]{1,0:T(8,128)(2,1)} %bitcast.6, bf16[6,2048]{1,0:T(8,128)(2,1)} %ri_hbm.1, bf16[8192,1024]{1,0:T(8,128)(2,1)} %bitcast.4, bf16[1024,768]{1,0:T(8,128)(2,1)} %bitcast.5, bf16[2048,1024]{1,0:T(8,128)(2,1)} %ii_hbm.1), custom_call_target="tpu_custom_call" | custom-call | tf_op jit(solution)/shard_map/pallas_call | solution.py:341
  53.8 1.6 %shard_map.78 = (bf16[48,1024]{1,0:T(8,128)(2,1)}, bf16[6,8192]{1,0:T(8,128)(2,1)}) custom-call(bf16[48,1024]{1,0:T(8,128)(2,1)} %get-tuple-element.6.a_hbm, bf16[6,8192]{1,0:T(8,128)(2,1)} %get-tuple-element.7.b_hbm), custom_call_target="tpu_custom_call" | custom-call | tf_op jit(solution)/shard_map/pallas_call | solution.py:350
